TPU v7x, 32 devices: a whole 2x2x4 slice. The times are simulated.
32 devices in a mesh: copies: 2 (over y), grid: 4 (over z), slab: 4 (over x, core).
Axes of the slice: x: 2, y: 2, z: 4, core: 2. Of those that a mesh axis runs over, the one named last changes fastest.
Arguments:
- field: float32 [8, 128, 64, 128], P(('copies', 'grid'), 'slab'), parts along dimension 0, may hold values from -6 to 6
- levels: int32 [8, 5], P(('copies', 'grid')), parts along dimension 0, may hold values from 1 to 3
- owner: int32 [256], P('copies'), parts along dimension 0, may hold values from 0 to 127, each once
Outputs:
- combined: float32 [256, 64, 128], P(('copies', 'grid'), 'slab'), parts along dimension 0
There are 2 independent parts, one for each index of `copies`. A program takes and returns all parts, laid end to end along the dimension named above; each array names one. Nothing has to cross between parts.
All inputs are finite; a program needn't handle non-finite values.
Results may differ from a plain program's by a relative error of at most 0.0003.
Values sent between devices are 32-bit elements; how exact they have to be, the bound alone decides.
A program may use at most 64 MiB of HBM per device.

v0:
```python
import functools
import math

import jax
import jax.numpy as jnp
from jax import lax
from jax.experimental import pallas as pl
from jax.experimental.pallas import tpu as pltpu
from jax.sharding import PartitionSpec as P

N1 = 2
N2 = 8
N3 = 4
STEPS = 4
SUB = 8
CHUNK = 2
ROOT_LAG = 3
OUT_LAG = 7
RS_LAG = 2
WAVE_LAG = 3
LOW = STEPS
HIGH = STEPS + 1

ADVECT = 0.08
DIFFUSE = 0.03
MESH = pl.DeviceIdType.MESH


def advance_row(u, back0, ahead0, coef):
    adv, dif, adv_sum, dif_sum = coef
    tiles = u.shape[0]
    sub = lax.broadcasted_iota(jnp.int32, u.shape, 1)
    inner = sub % N3
    back3 = jnp.where(inner == 0, pltpu.roll(u, SUB - N3 + 1, 1), pltpu.roll(u, 1, 1))
    ahead3 = jnp.where(inner == N3 - 1, pltpu.roll(u, N3 - 1, 1), pltpu.roll(u, SUB - 1, 1))
    turned = pltpu.roll(u, N3, 1)
    half = tiles // N1
    parts = [turned[n * half:(n + 1) * half] for n in range(N1)]
    before = jnp.concatenate([x for p in parts for x in (p[half - 1:], p[:half - 1])], axis=0)
    after = jnp.concatenate([x for p in parts for x in (p[1:], p[:1])], axis=0)
    back2 = jnp.where(sub < N3, before, turned)
    ahead2 = jnp.where(sub < N3, turned, after)
    other = jnp.concatenate([u[half:], u[:half]], axis=0)
    back4 = pltpu.roll(u, 1, 2)
    ahead4 = pltpu.roll(u, u.shape[2] - 1, 2)
    upwind = (adv[0] * back0 + adv[1] * other + adv[2] * back2 + adv[3] * back3 + adv[4] * back4
              - adv_sum * u)
    spread = (dif[0] * (back0 + ahead0) + (2.0 * dif[1]) * other + dif[2] * (back2 + ahead2)
              + dif[3] * (back3 + ahead3) + dif[4] * (back4 + ahead4) - dif_sum * u)
    return u + (1.0 + 0.5 * jnp.tanh(u)) * upwind + spread


def kernel(sizes, levels, owner, u_in, out, first, second, ext_s, terms, from_left, from_right,
           final, whole, rs_left, rs_right, rs_send,
           h_send, h_recv, up_send, l_recv, r_recv, dl_send, dr_send, d_recv, g_send, g_recv,
           a_send, a_recv, rs_ssem, rsl_recv, rsr_recv, in_sem):
    Z, S, rows, count = sizes
    z = lax.axis_index("grid")
    s = lax.axis_index("slab")
    nxt, prv = lax.rem(s + 1, S), lax.rem(s + S - 1, S)
    ext = rows + LOW + HIGH
    chunks = rows // CHUNK
    pairs = chunks // 2
    tiles_out = whole.shape[1]
    owned = count // Z
    piece = rs_left.shape[2]
    pieces = owned // piece

    def remote(src, dst, ssem, rsem, **where):
        return pltpu.make_async_remote_copy(src_ref=src, dst_ref=dst, send_sem=ssem, recv_sem=rsem,
                                            device_id=where, device_id_type=MESH)

    groups = rows // 4
    loaded = pltpu.make_async_copy(u_in, first.at[0, pl.ds(LOW, rows)], in_sem)
    loaded.start()
    vec = [levels[0, d] for d in range(5)]
    scales = [lax.shift_left(jnp.int32(1), v).astype(jnp.float32) * 0.125 for v in vec]
    adv = [ADVECT * x for x in scales]
    dif = [DIFFUSE * (x * x) for x in scales]
    coef = (adv, dif, sum(adv[1:], adv[0]), 2.0 * sum(dif[1:], dif[0]))
    size = jnp.float32(1.0 / math.sqrt(Z))
    weight = jnp.where(sum(vec[1:], vec[0]) % 2 == 0, size, -size)
    keep_mid, keep_fine = [jnp.where(3 - t <= vec[0], jnp.float32(1.0), jnp.float32(0.0)) for t in (1, 0)]

    barrier = pltpu.get_barrier_semaphore()
    for off in range(1, S):
        pl.semaphore_signal(barrier, inc=1, device_id={"slab": lax.rem(s + off, S)}, device_id_type=MESH)

    @pl.when(z > 0)
    def _():
        pl.semaphore_signal(barrier, inc=1, device_id={"grid": z - 1}, device_id_type=MESH)

    @pl.when(z < Z - 1)
    def _():
        pl.semaphore_signal(barrier, inc=1, device_id={"grid": z + 1}, device_id_type=MESH)

    pl.semaphore_wait(barrier, S - 1 + jnp.where(z > 0, 1, 0) + jnp.where(z < Z - 1, 1, 0))

    def wave(bufs, g, fresh):
        for k in range(1, STEPS + 1):
            low = jnp.where(fresh, 4 * g + k, 4 * g + 9 - k)

            @pl.loop(low, 4 * g + 9 - k)
            def _(e):
                bufs[k, e] = advance_row(bufs[k - 1, e], bufs[k - 1, e - 1], bufs[k - 1, e + 1], coef)

            @pl.loop(0, 2)
            def _(n):
                for e in [4 * g + 9 - k + 2 * n + i for i in range(2)]:
                    bufs[k, e] = advance_row(bufs[k - 1, e], bufs[k - 1, e - 1], bufs[k - 1, e + 1], coef)

    def make_terms(bufs, g, dst):
        r = 4 * g
        u0, u1, u2, u3, u4 = [bufs[STEPS, LOW + r + k] for k in range(5)]
        dst[r] = weight * u0
        dst[r + 1] = (weight * keep_fine) * (u1 - 0.5 * (u0 + u2))
        dst[r + 2] = (weight * keep_mid) * (u2 - 0.5 * (u0 + u4))
        dst[r + 3] = (weight * keep_fine) * (u3 - 0.5 * (u2 + u4))

    up = remote(first.at[0, pl.ds(rows, LOW)], first.at[0, pl.ds(0, LOW)], h_send.at[0], h_recv.at[0], slab=nxt)
    loaded.wait()
    down = remote(first.at[0, pl.ds(LOW, HIGH)], first.at[0, pl.ds(LOW + rows, HIGH)], h_send.at[1], h_recv.at[1], slab=prv)
    up.start()
    down.start()

    up.wait()
    down.wait()

    roots = (Z // 2 - 1, Z // 2)

    def at(position):
        return lax.rem(position + chunks - LOW // CHUNK, chunks)

    def span(c):
        return pl.ds(c * CHUNK, CHUNK)

    def shifted(c):
        return pl.ds(LOW + c * CHUNK, CHUNK)

    def to_right(c):
        return remote(terms.at[span(c)], from_left.at[span(c)], up_send.at[c], l_recv.at[c], grid=lax.rem(z + 1, Z))

    def to_left(c):
        return remote(terms.at[span(c)], from_right.at[span(c)], up_send.at[c], r_recv.at[c],
                      grid=lax.rem(z + Z - 1, Z))

    def result_right(c):
        return remote(ext_s.at[shifted(c)], ext_s.at[shifted(c)], dr_send.at[c], d_recv.at[c], grid=lax.rem(z + 1, Z))

    def result_left(c):
        return remote(ext_s.at[shifted(c)], ext_s.at[shifted(c)], dl_send.at[c], d_recv.at[c],
                      grid=lax.rem(z + Z - 1, Z))

    def add_in(c, other):
        for k in range(CHUNK):
            terms[c * CHUNK + k] += other[c * CHUNK + k]

    def inward(c, root):
        @pl.when(z < root)
        def _():
            @pl.when(z > 0)
            def _():
                to_right(c).wait_recv()
                add_in(c, from_left)
            to_right(c).start()

        @pl.when(z > root)
        def _():
            @pl.when(z < Z - 1)
            def _():
                to_left(c).wait_recv()
                add_in(c, from_right)
            to_left(c).start()

    def at_root(c, root):
        @pl.when(z == root)
        def _():
            if root > 0:
                to_right(c).wait_recv()
                add_in(c, from_left)
            if root < Z - 1:
                to_left(c).wait_recv()
                add_in(c, from_right)
            for k in range(CHUNK):
                ext_s[LOW + c * CHUNK + k] = terms[c * CHUNK + k]
            if root > 0:
                result_left(c).start()
            if root < Z - 1:
                result_right(c).start()

    def outward(c, root):
        @pl.when(z < root)
        def _():
            result_right(c).wait_recv()

            @pl.when(z > 0)
            def _():
                result_left(c).start()

        @pl.when(z > root)
        def _():
            result_left(c).wait_recv()

            @pl.when(z < Z - 1)
            def _():
                result_right(c).start()

    halo_up = remote(ext_s.at[pl.ds(rows, LOW)], ext_s.at[pl.ds(0, LOW)], g_send.at[0], g_recv.at[0], slab=nxt)
    halo_down = remote(ext_s.at[pl.ds(LOW, HIGH)], ext_s.at[pl.ds(LOW + rows, HIGH)], g_send.at[1], g_recv.at[1],
                       slab=prv)
    root_lag, out_lag = ROOT_LAG, OUT_LAG
    edge = out_lag + (LOW // CHUNK + -(-HIGH // CHUNK) - 1) // 2

    def restart(m):
        e = 4 * m
        s0, s1, s2, s3, s4 = [ext_s[e + k] for k in range(5)]
        mid = 0.5 * (s0 + s4) + keep_mid * s2
        second[0, e] = s0
        second[0, e + 1] = 0.5 * (s0 + mid) + keep_fine * s1
        second[0, e + 2] = mid
        second[0, e + 3] = 0.5 * (mid + s4) + keep_fine * s3
        second[0, e + 4] = s4

    def exchange(off, g):
        peer = lax.rem(s + off, S)
        return remote(final.at[pl.ds(4 * g, 4), pl.ds(peer * tiles_out, tiles_out)],
                      whole.at[pl.ds(s * rows + 4 * g, 4)],
                      a_send.at[off - 1, g], a_recv.at[off - 1, g], slab=peer)

    def arrival(off, g):
        peer = lax.rem(s + S - off, S)
        return remote(final.at[pl.ds(4 * g, 4), pl.ds(peer * tiles_out, tiles_out)],
                      whole.at[pl.ds(peer * rows + 4 * g, 4)],
                      a_send.at[off - 1, g], a_recv.at[off - 1, g], slab=peer)

    last = pairs + out_lag
    wave_lag = out_lag + WAVE_LAG

    @pl.loop(0, max(last, groups + wave_lag))
    def _(j):
        @pl.when(j < pairs)
        def _():
            g = lax.rem(j + groups - 1, groups)
            wave(first, g, j < 2)
            make_terms(first, g, terms)
            for k, root in enumerate(roots):
                inward(at(2 * j + k), root)

        @pl.when((j >= root_lag) & (j < pairs + root_lag))
        def _():
            for k, root in enumerate(roots):
                at_root(at(2 * (j - root_lag) + k), root)

        @pl.when((j >= out_lag) & (j < last))
        def _():
            for k, root in enumerate(roots):
                outward(at(2 * (j - out_lag) + k), root)

        @pl.when(j == edge)
        def _():
            halo_up.start()
            halo_down.start()

        @pl.when(j == wave_lag)
        def _():
            halo_up.wait()
            halo_down.wait()
            restart(0)
            restart(1)

        @pl.when((j >= wave_lag) & (j < groups + wave_lag))
        def _():
            g = j - wave_lag
            restart(g + 2)
            wave(second, g, g == 0)
            make_terms(second, g, final)
            for off in range(1, S):
                exchange(off, g).start()
            for k in range(4):
                whole[s * rows + 4 * g + k] = final[4 * g + k, pl.ds(s * tiles_out, tiles_out)]

    @pl.loop(0, chunks)
    def _(c):
        for k, root in enumerate(roots):
            @pl.when(((c + LOW // CHUNK) % 2 == k) & (z != root))
            def _():
                to_right(c).wait_send()

            @pl.when(((c + LOW // CHUNK) % 2 == k) & (z <= root) & (z > 0))
            def _():
                result_left(c).wait_send()

            @pl.when(((c + LOW // CHUNK) % 2 == k) & (z >= root) & (z < Z - 1))
            def _():
                result_right(c).wait_send()

    @pl.loop(0, groups)
    def _(g):
        for off in range(1, S):
            arrival(off, g).wait_recv()

    for spacing in [1 << t for t in range(2, count.bit_length() - 1)]:
        for i in range(spacing, count, 2 * spacing):
            whole[i] = whole[i] - 0.5 * (whole[i - spacing] + whole[(i + spacing) % count])

    def rs_right_copy(k, p):
        return remote(rs_send.at[k, p], rs_left.at[k, p], rs_ssem.at[k, p], rsl_recv.at[k, p], grid=lax.rem(z + 1, Z))

    def rs_left_copy(k, p):
        return remote(rs_send.at[k, p], rs_right.at[k, p], rs_ssem.at[k, p], rsr_recv.at[k, p],
                      grid=lax.rem(z + Z - 1, Z))

    def own(k, p, r):
        return whole[owner[k * owned + p * piece + r]]

    steps = (Z - 1) * pieces

    @pl.loop(0, steps + (Z - 1) * RS_LAG)
    def _(j):
        jr = j - RS_LAG * z
        inside_r = (jr >= 0) & (jr < steps)
        jr = jnp.clip(jr, 0, steps - 1)
        p = jr % pieces
        k = Z - 1 - jr // pieces

        @pl.when(inside_r & (k > z))
        def _():
            @pl.loop(0, piece)
            def _(r):
                rs_send[k, p, r] = own(k, p, r)

            @pl.when(z > 0)
            def _():
                rs_right_copy(k, p).wait_recv()

                @pl.loop(0, piece)
                def _(r):
                    rs_send[k, p, r] += rs_left[k, p, r]
            rs_right_copy(k, p).start()

        jl = j - RS_LAG * (Z - 1 - z)
        inside_l = (jl >= 0) & (jl < steps)
        jl = jnp.clip(jl, 0, steps - 1)
        q = jl % pieces
        n = jl // pieces

        @pl.when(inside_l & (n < z))
        def _():
            @pl.loop(0, piece)
            def _(r):
                rs_send[n, q, r] = own(n, q, r)

            @pl.when(z < Z - 1)
            def _():
                rs_left_copy(n, q).wait_recv()

                @pl.loop(0, piece)
                def _(r):
                    rs_send[n, q, r] += rs_right[n, q, r]
            rs_left_copy(n, q).start()

    @pl.loop(0, pieces)
    def _(p):
        @pl.loop(0, piece)
        def _(r):
            out[p * piece + r] = own(z, p, r)

        @pl.when(z > 0)
        def _():
            rs_right_copy(z, p).wait_recv()

            @pl.loop(0, piece)
            def _(r):
                out[p * piece + r] += rs_left[z, p, r]

        @pl.when(z < Z - 1)
        def _():
            rs_left_copy(z, p).wait_recv()

            @pl.loop(0, piece)
            def _(r):
                out[p * piece + r] += rs_right[z, p, r]

    @pl.loop(0, groups)
    def _(g):
        for off in range(1, S):
            exchange(off, g).wait_send()

    @pl.loop(0, Z)
    def _(k):
        @pl.when(k != z)
        def _():
            @pl.loop(0, pieces)
            def _(p):
                rs_right_copy(k, p).wait_send()


def local(field, levels, owner):
    _, rows, flat, lanes = field.shape
    Z, S = lax.axis_size("grid"), lax.axis_size("slab")
    count = owner.shape[0]
    tiles = flat // SUB
    tiles_out = tiles // S
    owned = count // Z
    piece = min(owned, 8)
    ext = rows + LOW + HIGH
    chunks = rows // CHUNK
    u = field[0].reshape(rows, tiles, SUB, lanes)
    tail = (tiles, SUB, lanes)
    tail_out = (tiles_out, SUB, lanes)
    f32 = jnp.float32
    vmem = lambda *shape: pltpu.VMEM(shape, f32)
    sems = lambda *shape: pltpu.SemaphoreType.DMA(shape)
    pieces = owned // piece
    result = pl.pallas_call(
        functools.partial(kernel, (Z, S, rows, count)),
        out_shape=jax.ShapeDtypeStruct((owned,) + tail_out, f32),
        in_specs=[pl.BlockSpec(memory_space=pltpu.SMEM), pl.BlockSpec(memory_space=pltpu.SMEM),
                  pl.BlockSpec(memory_space=pl.ANY)],
        out_specs=pl.BlockSpec(memory_space=pltpu.VMEM),
        scratch_shapes=[
            vmem(STEPS + 1, ext, *tail), vmem(STEPS + 1, ext, *tail), vmem(ext, *tail),
            vmem(rows, *tail), vmem(rows, *tail), vmem(rows, *tail),
            vmem(rows, *tail), vmem(count, *tail_out),
            vmem(Z, pieces, piece, *tail_out), vmem(Z, pieces, piece, *tail_out), vmem(Z, pieces, piece, *tail_out),
            sems(2), sems(2), sems(chunks), sems(chunks), sems(chunks), sems(chunks), sems(chunks), sems(chunks),
            sems(2), sems(2), sems(S - 1, rows // 4), sems(S - 1, rows // 4),
            sems(Z, pieces), sems(Z, pieces), sems(Z, pieces), pltpu.SemaphoreType.DMA,
        ],
        compiler_params=pltpu.CompilerParams(collective_id=0, has_side_effects=True,
                                             vmem_limit_bytes=40 * 1024 * 1024),
    )(levels, owner, u)
    return result.reshape(owned, flat // S, lanes)


def solution(mesh):
    in_specs = (P(("copies", "grid"), "slab", None, None), P(("copies", "grid"), None), P("copies"))
    out_specs = P(("copies", "grid"), "slab", None)
    return jax.shard_map(local, mesh=mesh, in_specs=in_specs, out_specs=out_specs, check_vma=False)
```

profile of v0, /device:TPU:0, one launch (start us, length us, event | category | flops | bytes accessed | tf_op | source)
XLA Modules:
  0.0 86.5 jit_solution(4121697384663152898)
XLA Ops:
  0.0 0.0 copy-start.2
  0.0 0.0 copy-start.1
  0.0 0.7 copy-done.2
  0.7 0.0 copy-done.1
  0.7 0.0 copy-start
  0.7 1.2 %copy-done = f32[1,32,64,128]{3,2,1,0:T(8,128)S(1)} copy-done((f32[1,32,64,128]{3,2,1,0:T(8,128)S(1)}, f32[1,32,64,128]{3,2,1,0:T(8,128)}, u32[]{:S(2)}) %copy-start) | copy-done | bytes 1048600
  1.9 83.9 %shard_map.37 = f32[32,2,8,128]{3,2,1,0:T(8,128)S(1)} custom-call(s32[1,5]{1,0:T(1,128)S(1)} %copy-done.1, s32[128]{0:T(128)S(1)} %copy-done.2, f32[32,8,8,128]{3,2,1,0:T(8,128)S(1)} %bitcast.2), custom_call_target="tpu_custom_call" | custom-call | tf_op jit(solution)/shard_map/pallas_call | solution.py:415
  85.8 0.7 copy.5
Async XLA Ops:
  0.0 0.7 copy-start.2
  0.0 0.7 copy-start.1
  0.7 1.2 %copy-start = (f32[1,32,64,128]{3,2,1,0:T(8,128)S(1)}, f32[1,32,64,128]{3,2,1,0:T(8,128)}, u32[]{:S(2)}) copy-start(f32[1,32,64,128]{3,2,1,0:T(8,128)} %param.3) | copy-start | bytes 3145732
where the time goes:
time: 86.7 us; the launch traced here: 86.5 us
  Pallas kernels  83.9 us (97%)
  local copies, waits for them, and re-layouts  2.6 us (3%)
    pallas_call x1, Pallas kernels, local(): pl.pallas_call(functools.partial(kernel, (Z, S, rows, count)), out_shape=...  83.9 us
    unnamed x7, local copies, waits for them, and re-layouts  2.6 us

commit v1 on v0

v1 whole, which is shorter than its diff:
```python
import functools
import math

import jax
import jax.numpy as jnp
from jax import lax
from jax.experimental import pallas as pl
from jax.experimental.pallas import tpu as pltpu
from jax.sharding import PartitionSpec as P

N1 = 2
N2 = 8
N3 = 4
STEPS = 4
LOW = STEPS
HIGH = STEPS + 1
EDGE = STEPS + 1
OFF = 8
RS_LAG = 1
C2_LAG = 0
SWAP_LAG = 1
PLANE_LAG = 1
CHAIN_LAG = 1

ADVECT = 0.08
DIFFUSE = 0.03
MESH = pl.DeviceIdType.MESH


def coefficients(scales, descending):
    adv = [ADVECT * x for x in scales]
    dif = [DIFFUSE * (x * x) for x in scales]
    flag = jnp.where(descending, jnp.float32(1.0), jnp.float32(0.0))
    behind, front = (1.0 - flag) * adv[0], flag * adv[0]
    return [behind, front, adv[1], adv[2], adv[3], adv[4], sum(adv[1:], adv[0]),
            dif[0], 2.0 * dif[1], dif[2], dif[3], dif[4], 1.0 - 2.0 * sum(dif[1:], dif[0])]


def advance_row(behind, u, front, coef):
    c_behind, c_front, a1, a2, a3, a4, a_sum, d0, d1, d2, d3, d4, d_own = coef
    back2 = [pltpu.roll(x, 1, 0) for x in u]
    ahead2 = [pltpu.roll(x, N2 - 1, 0) for x in u]
    back4 = [pltpu.roll(x, 1, 1) for x in u]
    ahead4 = [pltpu.roll(x, x.shape[1] - 1, 1) for x in u]
    both3 = [None] * (N1 * N3)
    for n in range(N1):
        for m in range(N3 // 2):
            pair = d3 * (u[n * N3 + m] + u[n * N3 + m + 2])
            both3[n * N3 + m + 1] = both3[n * N3 + (m + 3) % N3] = pair
    out = []
    for t in range(N1 * N3):
        n, m = divmod(t, N3)
        other = u[(N1 - 1 - n) * N3 + m]
        back3 = u[n * N3 + (m + N3 - 1) % N3]
        upwind = (c_behind * behind[t] + c_front * front[t] + a1 * other + a2 * back2[t] + a3 * back3
                  + a4 * back4[t] - a_sum * u[t])
        spread = (d0 * (behind[t] + front[t]) + d1 * other + d2 * (back2[t] + ahead2[t]) + both3[t]
                  + d4 * (back4[t] + ahead4[t]) + d_own * u[t])
        out.append(spread + (1.0 + 0.5 * jnp.tanh(u[t])) * upwind)
    return out


TILES = N1 * N3


def get(ref, *index):
    return [ref[(*index, t)] for t in range(TILES)]


def put(ref, row, *index):
    for t in range(TILES):
        ref[(*index, t)] = row[t]


def spots():
    return [pl.ds(n * N2 * N3 + m, N2, stride=N3) for n in range(N1) for m in range(N3)]


def warm_up(carry, rows, coef):
    for k in range(STEPS):
        put(carry, rows[-2], k, 0)
        put(carry, rows[-1], k, 1)
        rows = [advance_row(rows[i], rows[i + 1], rows[i + 2], coef) for i in range(len(rows) - 2)]
    put(carry, rows[-1], STEPS, 1)


def march(carry, fresh, coef):
    for k in range(STEPS):
        seq = [get(carry, k, 0), get(carry, k, 1)] + fresh
        put(carry, fresh[-2], k, 0)
        put(carry, fresh[-1], k, 1)
        fresh = [advance_row(seq[i], seq[i + 1], seq[i + 2], coef) for i in range(4)]
    old = get(carry, STEPS, 1)
    put(carry, fresh[-1], STEPS, 1)
    return [old] + fresh


def surpluses(m, first, last, mid, fine):
    coarse = [first * a + last * b for a, b in zip(m[0], m[4])]
    one = [fine * (b - 0.5 * (a + c)) for a, b, c in zip(m[0], m[1], m[2])]
    two = [mid * (b - 0.5 * (a + c)) for a, b, c in zip(m[0], m[2], m[4])]
    three = [fine * (b - 0.5 * (a + c)) for a, b, c in zip(m[2], m[3], m[4])]
    return coarse, one, two, three


def kernel(sizes, levels, owner, u_in, out, raw, carry, terms, arrived, h_terms, h_arrived, sums, carry2, part, swapped,
           fin, whole, table, lv_up, lv_down, lv_up_in, lv_down_in,
           ssem, rsem, c_send, c_recv, p_send, p_recv, x_send, x_recv, up_send, up_recv, dn_send, dn_recv,
           h_send, h_recv, in_sem):
    Z, S, rows, count, lanes = sizes
    flat = N1 * N2 * N3
    width = flat // S
    chips = S // 2
    groups = rows // 4
    owned = count // Z
    local_grids = Z // 2
    z = lax.axis_index("grid")
    s = lax.axis_index("slab")
    core = lax.rem(s, 2)
    chip = lax.div(s, 2)
    partner = s + 1 - 2 * core
    nxt, prv = lax.rem(s + 1, S), lax.rem(s + S - 1, S)
    up_z, down_z = jnp.minimum(z + 1, Z - 1), jnp.maximum(z - 1, 0)
    descending = core == 0
    to_zero = lax.rem(s + 1, 4) <= 1
    hop = jnp.where(to_zero, Z - 1 - z, z)
    h_hop = Z - 1 - hop
    main_z = jnp.where(to_zero, down_z, up_z)
    halo_z = jnp.where(to_zero, up_z, down_z)
    at_end = (z == 0) | (z == Z - 1)
    is_main = hop == Z - 1
    region = jnp.where(is_main, s, partner)
    region_desc = lax.rem(region, 2) == 0
    neighbour = jnp.where(region_desc, lax.rem(region + S - 1, S), lax.rem(region + 1, S))

    def remote(src, dst, send, recv, **where):
        return pltpu.make_async_remote_copy(src_ref=src, dst_ref=dst, send_sem=send, recv_sem=recv,
                                            device_id=where, device_id_type=MESH)

    def group_of(desc, j):
        return jnp.where(desc, groups - 1 - j, j)

    def row_of(desc, i):
        return jnp.where(desc, rows - i, i)

    loaded = pltpu.make_async_copy(u_in, raw.at[pl.ds(LOW, rows)], in_sem)
    loaded.start()
    vec = [levels[0, d] for d in range(5)]
    scales = [lax.shift_left(jnp.int32(1), v).astype(jnp.float32) * 0.125 for v in vec]
    size = jnp.float32(1.0 / math.sqrt(Z))
    weight = jnp.where(sum(vec[1:], vec[0]) % 2 == 0, size, -size)

    barrier = pltpu.get_barrier_semaphore()
    for off in range(1, S):
        pl.semaphore_signal(barrier, inc=1, device_id={"slab": lax.rem(s + off, S)}, device_id_type=MESH)

    @pl.when(z > 0)
    def _():
        pl.semaphore_signal(barrier, inc=1, device_id={"grid": down_z}, device_id_type=MESH)

    @pl.when(z < Z - 1)
    def _():
        pl.semaphore_signal(barrier, inc=1, device_id={"grid": up_z}, device_id_type=MESH)

    sub = lax.broadcasted_iota(jnp.int32, (8, lanes), 0)
    tile = jnp.zeros((8, lanes), jnp.float32)
    for d, value in enumerate(scales + [weight]):
        tile = jnp.where(sub == d, value, tile)
    for g in range(Z):
        lv_up[g] = tile
        lv_down[g] = tile
    coef = coefficients(scales, descending)
    keep_mid, keep_fine = [jnp.where(3 - t <= vec[0], jnp.float32(1.0), jnp.float32(0.0)) for t in (1, 0)]
    first_w = jnp.where(descending, 0.0 * weight, weight)
    last_w = jnp.where(descending, weight, 0.0 * weight)

    pl.semaphore_wait(barrier, S - 1 + jnp.where(z > 0, 1, 0) + jnp.where(z < Z - 1, 1, 0))

    up = remote(u_in.at[pl.ds(rows - LOW, LOW)], raw.at[pl.ds(0, LOW)], h_send.at[0], h_recv.at[0], slab=nxt)
    down = remote(u_in.at[pl.ds(0, HIGH)], raw.at[pl.ds(LOW + rows, HIGH)], h_send.at[1], h_recv.at[1], slab=prv)
    up.start()
    down.start()
    send_levels_up = remote(lv_up, lv_up_in, h_send.at[2], h_recv.at[2], grid=up_z)
    send_levels_down = remote(lv_down, lv_down_in, h_send.at[3], h_recv.at[3], grid=down_z)

    @pl.when(z == 0)
    def _():
        send_levels_up.start()

    @pl.when(z == Z - 1)
    def _():
        send_levels_down.start()

    loaded.wait()

    @pl.when(descending)
    def _():
        down.wait_recv()

    @pl.when(jnp.logical_not(descending))
    def _():
        up.wait_recv()

    def raw_row(i):
        r = LOW + row_of(descending, i)
        return [raw[r, spot] for spot in spots()]

    warm_up(carry, [raw_row(i) for i in range(-STEPS, STEPS + 1)], coef)

    def first_cycle(j):
        m = march(carry, [raw_row(4 * j + 5 + i) for i in range(4)], coef)
        r = 4 * group_of(descending, j)
        coarse, one, two, three = surpluses(m, first_w, last_w, weight * keep_mid, weight * keep_fine)
        put(terms, coarse, r)
        put(terms, one, r + jnp.where(descending, 3, 1))
        put(terms, two, r + 2)
        put(terms, three, r + jnp.where(descending, 1, 3))

    def chunk(i):
        return pl.ds(4 * group_of(descending, i), 4)

    def main_copy(i):
        return remote(terms.at[chunk(i)], arrived.at[chunk(i)], ssem.at[i], rsem.at[i], grid=main_z)

    halo_copy = remote(h_terms, h_arrived, h_send.at[4], h_recv.at[4], grid=halo_z)

    def share_copy(i):
        where = pl.ds(OFF + 4 * group_of(region_desc, i), 4)
        return remote(sums.at[where], sums.at[where], c_send.at[i], c_recv.at[i], slab=partner)

    inner_at = OFF + jnp.where(region_desc, rows, -EDGE)
    outer_at = OFF + jnp.where(region_desc, -EDGE, rows)
    inner = pl.ds(inner_at, EDGE)
    outer = pl.ds(outer_at, EDGE)
    share_inner = remote(sums.at[inner], sums.at[inner], h_send.at[5], h_recv.at[5], slab=partner)
    swap_outer = remote(sums.at[pl.ds(OFF + jnp.where(region_desc, 0, rows - EDGE), EDGE)], sums.at[inner],
                        h_send.at[6], h_recv.at[6], slab=neighbour)
    share_outer = remote(sums.at[outer], sums.at[outer], h_send.at[7], h_recv.at[7], slab=partner)

    def cell(q, keeps):
        mid_keep, fine_keep = keeps
        c = [get(sums, OFF + row_of(region_desc, 4 * q + i)) for i in range(5)]
        mid = [0.5 * (a + b) + mid_keep * x for a, b, x in zip(c[0], c[4], c[2])]
        one = [0.5 * (a + b) + fine_keep * x for a, b, x in zip(c[0], mid, c[1])]
        three = [0.5 * (a + b) + fine_keep * x for a, b, x in zip(mid, c[4], c[3])]
        return [c[0], one, mid, three, c[4]]

    NC = 13

    def build_table():
        for n in range(local_grids):
            g = n + jnp.where(is_main, 0, local_grids)
            both = jnp.where(z == 0, 1.0, 0.0) * lv_down[g] + jnp.where(z == 0, 0.0, 1.0) * lv_up[g]
            lines = [jnp.broadcast_to(both[d:d + 1], (8, lanes)) for d in range(6)]
            values = coefficients(lines[:5], region_desc)
            w = lines[5]
            mid = jnp.where(lines[0] >= 0.5, 1.0, 0.0)
            fine = jnp.where(lines[0] >= 1.0, 1.0, 0.0)
            flag = jnp.where(region_desc, 1.0, 0.0)
            values = values + [mid, fine, (1.0 - flag) * w, flag * w, mid * w, fine * w]
            for k, v in enumerate(values):
                table[n, k] = v

    def table_of(n):
        values = [table[n, k] for k in range(NC + 6)]
        return values[:NC], values[NC:NC + 2], values[NC + 2:]

    def second_warm():
        for n in range(local_grids):
            c, keeps, _ = table_of(n)
            before, after = cell(-1, keeps), cell(0, keeps)
            warm_up(carry2.at[n], before[:4] + after, c)

    def second_cycle(i):
        total = None
        for n in range(local_grids):
            c, keeps, weights = table_of(n)
            m = march(carry2.at[n], cell(i + 1, keeps)[1:], c)
            rows4 = surpluses(m, *weights)
            total = rows4 if total is None else [[a + b for a, b in zip(x, y)] for x, y in zip(total, rows4)]
        r = 4 * group_of(region_desc, i)
        places = [r, r + jnp.where(region_desc, 3, 1), r + 2, r + jnp.where(region_desc, 1, 3)]
        for place, row in zip(places, total):
            for spot, value in zip(spots(), row):
                part[place, spot] = value

    def quarter(x, c):
        return pl.ds(pl.multiple_of((2 * x + c) * width, 8), width)

    def swap_copy(i, x):
        where = pl.ds(4 * group_of(region_desc, i), 4)
        return remote(part.at[where, quarter(x, 1 - core)], swapped.at[where, x], p_send.at[i, x], p_recv.at[i, x],
                      slab=partner)

    def plane_copy(i, x):
        r = 4 * group_of(region_desc, i)
        return remote(fin.at[pl.ds(r, 4), x], whole.at[pl.ds(region * rows + r, 4)],
                      x_send.at[i, x], x_recv.at[i, chip], slab=2 * x + core)

    def slab_from(x, base):
        return 2 * x + (x % 2 if base == 0 else 1 - x % 2)

    def lot(i, x, base):
        m = slab_from(x, base)
        g = groups - 1 - i if m % 2 == 0 else i
        return pl.ds(m * rows + 4 * g, 4)

    def plane_arrival(i, x, base):
        return remote(fin.at[pl.ds(0, 4), 0], whole.at[lot(i, x, base)], x_send.at[i, x], x_recv.at[i, x],
                      slab=2 * x + core)

    def up_copy(i, x):
        return remote(whole.at[lot(i, x, 0)], whole.at[lot(i, x, 0)], up_send.at[i, x], up_recv.at[i, x], grid=up_z)

    def down_copy(i, x):
        return remote(whole.at[lot(i, x, 1)], whole.at[lot(i, x, 1)], dn_send.at[i, x], dn_recv.at[i, x],
                      grid=down_z)

    reach = (Z - 1) * RS_LAG
    start2 = reach + C2_LAG + 2
    swap_at = start2 + SWAP_LAG
    plane_at = swap_at + PLANE_LAG
    last = plane_at + (Z - 1) * CHAIN_LAG + groups

    @pl.loop(0, last)
    def _(j):
        @pl.when(j == groups - 2)
        def _():
            @pl.when(descending)
            def _():
                up.wait_recv()

            @pl.when(jnp.logical_not(descending))
            def _():
                down.wait_recv()

        @pl.when(j < groups)
        def _():
            first_cycle(j)

            @pl.when(hop == 0)
            def _():
                main_copy(j).start()

        @pl.when(j == 1)
        def _():
            e = jnp.where(descending, rows - EDGE, 0)
            for k in range(EDGE):
                put(h_terms, get(terms, e + k), k)

            @pl.when(h_hop == 0)
            def _():
                halo_copy.start()

        @pl.when((z > 0) & (j == z * RS_LAG))
        def _():
            send_levels_up.wait_recv()
            for g in range(Z):
                lv_up[g] = lv_up_in[g]
            lv_up[z] = tile

            @pl.when(z < Z - 1)
            def _():
                send_levels_up.start()

        @pl.when((z < Z - 1) & (j == (Z - 1 - z) * RS_LAG))
        def _():
            send_levels_down.wait_recv()
            for g in range(Z):
                lv_down[g] = lv_down_in[g]
            lv_down[z] = tile

            @pl.when(z > 0)
            def _():
                send_levels_down.start()

        @pl.when((h_hop > 0) & (j == 1 + h_hop * RS_LAG))
        def _():
            halo_copy.wait_recv()

            @pl.when(h_hop < Z - 1)
            def _():
                for k in range(EDGE):
                    put(h_terms, [a + b for a, b in zip(get(h_terms, k), get(h_arrived, k))], k)
                halo_copy.start()

            @pl.when(h_hop == Z - 1)
            def _():
                for k in range(EDGE):
                    put(sums, [a + b for a, b in zip(get(h_terms, k), get(h_arrived, k))], inner_at + k)
                share_inner.start()

        b = j - hop * RS_LAG

        @pl.when((hop > 0) & (b >= 0) & (b < groups))
        def _():
            main_copy(b).wait_recv()
            r = 4 * group_of(descending, b)

            @pl.when(hop < Z - 1)
            def _():
                for k in range(4):
                    put(terms, [a + c for a, c in zip(get(terms, r + k), get(arrived, r + k))], r + k)
                main_copy(b).start()

            @pl.when(hop == Z - 1)
            def _():
                for k in range(4):
                    put(sums, [a + c for a, c in zip(get(terms, r + k), get(arrived, r + k))], OFF + r + k)
                share_copy(b).start()

                @pl.when(b == groups - 1)
                def _():
                    swap_outer.start()

        i = j - start2

        @pl.when(at_end & (i == 0))
        def _():
            build_table()

            @pl.when(is_main)
            def _():
                share_inner.wait_recv()

            @pl.when(jnp.logical_not(is_main))
            def _():
                for k in range(min(2, groups)):
                    share_copy(k).wait_recv()
            second_warm()

        @pl.when(at_end & (i == groups - 2))
        def _():
            @pl.when(is_main)
            def _():
                swap_outer.wait_recv()
                share_outer.start()

            @pl.when(jnp.logical_not(is_main))
            def _():
                share_outer.wait_recv()

        @pl.when(at_end & (i >= 0) & (i < groups))
        def _():
            @pl.when(jnp.logical_not(is_main) & (i + 2 < groups))
            def _():
                share_copy(jnp.minimum(i + 2, groups - 1)).wait_recv()
            second_cycle(i)
            for x in range(chips):
                swap_copy(i, x).start()

        k = j - swap_at

        @pl.when(at_end & (k >= 0) & (k < groups))
        def _():
            r = 4 * group_of(region_desc, k)
            for x in range(chips):
                swap_copy(k, x).wait_recv()

                @pl.when(chip == x)
                def _():
                    for n in range(4):
                        whole[region * rows + r + n] = part[r + n, quarter(x, core)] + swapped[r + n, x]

                @pl.when(chip != x)
                def _():
                    for n in range(4):
                        fin[r + n, x] = part[r + n, quarter(x, core)] + swapped[r + n, x]
                    plane_copy(k, x).start()

        k2 = j - plane_at

        @pl.when((z == 0) & (k2 >= 0) & (k2 < groups))
        def _():
            for x in range(chips):
                @pl.when(chip != x)
                def _():
                    plane_arrival(k2, x, 0).wait_recv()
                up_copy(k2, x).start()

        @pl.when((z == Z - 1) & (k2 >= 0) & (k2 < groups))
        def _():
            for x in range(chips):
                @pl.when(chip != x)
                def _():
                    plane_arrival(k2, x, 1).wait_recv()
                down_copy(k2, x).start()

        f = k2 - z * CHAIN_LAG

        @pl.when((z > 0) & (f >= 0) & (f < groups))
        def _():
            for x in range(chips):
                up_copy(f, x).wait_recv()

                @pl.when(z < Z - 1)
                def _():
                    up_copy(f, x).start()

        d = k2 - (Z - 1 - z) * CHAIN_LAG

        @pl.when((z < Z - 1) & (d >= 0) & (d < groups))
        def _():
            for x in range(chips):
                down_copy(d, x).wait_recv()

                @pl.when(z > 0)
                def _():
                    down_copy(d, x).start()

    @pl.loop(0, groups)
    def _(i):
        @pl.when(hop < Z - 1)
        def _():
            main_copy(i).wait_send()

        @pl.when(at_end & is_main)
        def _():
            share_copy(i).wait_send()

        for x in range(chips):
            @pl.when(at_end)
            def _():
                swap_copy(i, x).wait_send()

            @pl.when(at_end & (chip != x))
            def _():
                plane_copy(i, x).wait_send()

            @pl.when(z < Z - 1)
            def _():
                up_copy(i, x).wait_send()

            @pl.when(z > 0)
            def _():
                down_copy(i, x).wait_send()

    up.wait_send()
    down.wait_send()

    @pl.when(h_hop < Z - 1)
    def _():
        halo_copy.wait_send()

    @pl.when(z < Z - 1)
    def _():
        send_levels_up.wait_send()

    @pl.when(z > 0)
    def _():
        send_levels_down.wait_send()

    @pl.when(at_end & is_main)
    def _():
        swap_outer.wait_send()
        share_outer.wait_send()

    @pl.when(at_end & jnp.logical_not(is_main))
    def _():
        share_inner.wait_send()

    for spacing in [1 << t for t in range(2, count.bit_length() - 1)]:
        for i in range(spacing, count, 2 * spacing):
            whole[i] = whole[i] - 0.5 * (whole[i - spacing] + whole[(i + spacing) % count])

    @pl.loop(0, owned)
    def _(r):
        out[r] = whole[owner[z * owned + r]]


def local(field, levels, owner):
    _, rows, flat, lanes = field.shape
    Z, S = lax.axis_size("grid"), lax.axis_size("slab")
    count = owner.shape[0]
    width = flat // S
    owned = count // Z
    groups = rows // 4
    chips = S // 2
    grids = Z // 2
    tail = (TILES, N2, lanes)
    vmem = lambda *shape: pltpu.VMEM(shape, jnp.float32)
    sems = lambda *shape: pltpu.SemaphoreType.DMA(shape)
    level_tiles = vmem(Z, 8, lanes)
    return pl.pallas_call(
        functools.partial(kernel, (Z, S, rows, count, lanes)),
        out_shape=jax.ShapeDtypeStruct((owned, width, lanes), jnp.float32),
        in_specs=[pl.BlockSpec(memory_space=pltpu.SMEM), pl.BlockSpec(memory_space=pltpu.SMEM),
                  pl.BlockSpec(memory_space=pl.ANY)],
        out_specs=pl.BlockSpec(memory_space=pltpu.VMEM),
        scratch_shapes=[
            vmem(rows + LOW + HIGH, flat, lanes), vmem(STEPS + 1, 2, *tail), vmem(rows, *tail), vmem(rows, *tail),
            vmem(EDGE, *tail), vmem(EDGE, *tail), vmem(OFF + rows + EDGE, *tail),
            vmem(grids, STEPS + 1, 2, *tail), vmem(rows, flat, lanes), vmem(rows, chips, width, lanes),
            vmem(rows, chips, width, lanes), vmem(count, width, lanes), vmem(grids, 19, 8, lanes),
            level_tiles, level_tiles, level_tiles, level_tiles,
            sems(groups), sems(groups), sems(groups), sems(groups), sems(groups, chips), sems(groups, chips),
            sems(groups, chips), sems(groups, chips), sems(groups, chips), sems(groups, chips),
            sems(groups, chips), sems(groups, chips), sems(8), sems(8), pltpu.SemaphoreType.DMA,
        ],
        compiler_params=pltpu.CompilerParams(collective_id=0, has_side_effects=True,
                                             vmem_limit_bytes=40 * 1024 * 1024),
    )(levels, owner, field[0])


def solution(mesh):
    in_specs = (P(("copies", "grid"), "slab", None, None), P(("copies", "grid"), None), P("copies"))
    out_specs = P(("copies", "grid"), "slab", None)
    return jax.shard_map(local, mesh=mesh, in_specs=in_specs, out_specs=out_specs, check_vma=False)
```

time: 86.7 us -> 72.6 us (0.84)
  Pallas kernels: 83.9 us -> 69.8 us
    pallas_call x1, Pallas kernels: 83.9 us -> 69.8 us  [local(): pl.pallas_call(functools.partial(kernel, (Z, S, rows, count, lanes)), out...]
where the time goes in v1:
time: 72.6 us; the launch traced here: 72.4 us
  Pallas kernels  69.8 us (96%)
  local copies, waits for them, and re-layouts  2.6 us (4%)
    pallas_call x1, Pallas kernels, local(): pl.pallas_call(functools.partial(kernel, (Z, S, rows, count, lanes)), out...  69.8 us
    unnamed x7, local copies, waits for them, and re-layouts  2.6 us

profile of v1, /device:TPU:0, one launch (start us, length us, event | category | flops | bytes accessed | tf_op | source)
XLA Modules:
  0.0 72.4 jit_solution(10142305472334496646)
XLA Ops:
  0.0 0.0 copy-start.2
  0.0 0.0 copy-start.1
  0.0 0.7 copy-done.2
  0.7 0.0 copy-done.1
  0.7 0.0 copy-start
  0.7 1.2 %copy-done = f32[1,32,64,128]{3,2,1,0:T(8,128)S(1)} copy-done((f32[1,32,64,128]{3,2,1,0:T(8,128)S(1)}, f32[1,32,64,128]{3,2,1,0:T(8,128)}, u32[]{:S(2)}) %copy-start) | copy-done | bytes 1048600
  1.9 69.8 %shard_map.37 = f32[32,16,128]{2,1,0:T(8,128)S(1)} custom-call(s32[1,5]{1,0:T(1,128)S(1)} %copy-done.1, s32[128]{0:T(128)S(1)} %copy-done.2, f32[32,64,128]{2,1,0:T(8,128)S(1)} %bitcast.1), custom_call_target="tpu_custom_call" | custom-call | tf_op jit(solution)/shard_map/pallas_call | solution.py:584
  71.7 0.7 copy.5
Async XLA Ops:
  0.0 0.7 copy-start.2
  0.0 0.7 copy-start.1
  0.7 1.2 %copy-start = (f32[1,32,64,128]{3,2,1,0:T(8,128)S(1)}, f32[1,32,64,128]{3,2,1,0:T(8,128)}, u32[]{:S(2)}) copy-start(f32[1,32,64,128]{3,2,1,0:T(8,128)} %param.3) | copy-start | bytes 3145732

commit v2 on v1

--- a/solution.py
+++ b/solution.py
@@ -12,15 +12,16 @@
 N2 = 8
 N3 = 4
 STEPS = 4
-LOW = STEPS
-HIGH = STEPS + 1
 EDGE = STEPS + 1
+WIDE = 2 * STEPS + 1
 OFF = 8
-RS_LAG = 1
-C2_LAG = 0
+PIECE = 2
+DIRECT = 8
+RS_LAG = 2
+C2_LAG = 1
 SWAP_LAG = 1
-PLANE_LAG = 1
-CHAIN_LAG = 1
+PLANE_LAG = 2
+CHAIN_LAG = 2
 
 ADVECT = 0.08
 DIFFUSE = 0.03
@@ -103,9 +104,9 @@
     return coarse, one, two, three
 
 
-def kernel(sizes, levels, owner, u_in, out, raw, carry, terms, arrived, h_terms, h_arrived, sums, carry2, part, swapped,
-           fin, whole, table, lv_up, lv_down, lv_up_in, lv_down_in,
-           ssem, rsem, c_send, c_recv, p_send, p_recv, x_send, x_recv, up_send, up_recv, dn_send, dn_recv,
+def kernel(sizes, levels_in, owner_in, u_in, out, levels, owner, raw, carry, terms, arrived, h_out, h_terms, h_arrived, o_terms, o_arrived,
+           sums, carry2, part, swapped, fin, whole, coarse, table, lv, lv_in,
+           ssem, rsem, c_send, c_recv, p_send, p_recv, x_send, x_recv, up_send, up_recv, dn_send, dn_recv, all_send,
            h_send, h_recv, in_sem):
     Z, S, rows, count, lanes = sizes
     flat = N1 * N2 * N3
@@ -124,14 +125,13 @@
     descending = core == 0
     to_zero = lax.rem(s + 1, 4) <= 1
     hop = jnp.where(to_zero, Z - 1 - z, z)
-    h_hop = Z - 1 - hop
     main_z = jnp.where(to_zero, down_z, up_z)
-    halo_z = jnp.where(to_zero, up_z, down_z)
     at_end = (z == 0) | (z == Z - 1)
     is_main = hop == Z - 1
     region = jnp.where(is_main, s, partner)
     region_desc = lax.rem(region, 2) == 0
-    neighbour = jnp.where(region_desc, lax.rem(region + S - 1, S), lax.rem(region + 1, S))
+    neighbour = jnp.where(descending, prv, nxt)
+    direct_from = min(DIRECT, groups)
 
     def remote(src, dst, send, recv, **where):
         return pltpu.make_async_remote_copy(src_ref=src, dst_ref=dst, send_sem=send, recv_sem=recv,
@@ -143,32 +143,36 @@
     def row_of(desc, i):
         return jnp.where(desc, rows - i, i)
 
-    loaded = pltpu.make_async_copy(u_in, raw.at[pl.ds(LOW, rows)], in_sem)
+    small = pltpu.make_async_copy(levels_in, levels, in_sem.at[1])
+    small.start()
+    loaded = pltpu.make_async_copy(u_in, raw.at[pl.ds(WIDE, rows)], in_sem.at[0])
     loaded.start()
+    owners = pltpu.make_async_copy(owner_in, owner, in_sem.at[2])
+    owners.start()
+    barrier = pltpu.get_barrier_semaphore()
+    for off in range(1, S):
+        pl.semaphore_signal(barrier, inc=1, device_id={"slab": lax.rem(s + off, S)}, device_id_type=MESH)
+
+    @pl.when(z > 0)
+    def _():
+        pl.semaphore_signal(barrier, inc=1, device_id={"grid": down_z}, device_id_type=MESH)
+
+    @pl.when(z < Z - 1)
+    def _():
+        pl.semaphore_signal(barrier, inc=1, device_id={"grid": up_z}, device_id_type=MESH)
+
+    small.wait()
     vec = [levels[0, d] for d in range(5)]
     scales = [lax.shift_left(jnp.int32(1), v).astype(jnp.float32) * 0.125 for v in vec]
     size = jnp.float32(1.0 / math.sqrt(Z))
     weight = jnp.where(sum(vec[1:], vec[0]) % 2 == 0, size, -size)
-
-    barrier = pltpu.get_barrier_semaphore()
-    for off in range(1, S):
-        pl.semaphore_signal(barrier, inc=1, device_id={"slab": lax.rem(s + off, S)}, device_id_type=MESH)
-
-    @pl.when(z > 0)
-    def _():
-        pl.semaphore_signal(barrier, inc=1, device_id={"grid": down_z}, device_id_type=MESH)
-
-    @pl.when(z < Z - 1)
-    def _():
-        pl.semaphore_signal(barrier, inc=1, device_id={"grid": up_z}, device_id_type=MESH)
 
     sub = lax.broadcasted_iota(jnp.int32, (8, lanes), 0)
     tile = jnp.zeros((8, lanes), jnp.float32)
     for d, value in enumerate(scales + [weight]):
         tile = jnp.where(sub == d, value, tile)
     for g in range(Z):
-        lv_up[g] = tile
-        lv_down[g] = tile
+        lv[g] = tile
     coef = coefficients(scales, descending)
     keep_mid, keep_fine = [jnp.where(3 - t <= vec[0], jnp.float32(1.0), jnp.float32(0.0)) for t in (1, 0)]
     first_w = jnp.where(descending, 0.0 * weight, weight)
@@ -176,53 +180,56 @@
 
     pl.semaphore_wait(barrier, S - 1 + jnp.where(z > 0, 1, 0) + jnp.where(z < Z - 1, 1, 0))
 
-    up = remote(u_in.at[pl.ds(rows - LOW, LOW)], raw.at[pl.ds(0, LOW)], h_send.at[0], h_recv.at[0], slab=nxt)
-    down = remote(u_in.at[pl.ds(0, HIGH)], raw.at[pl.ds(LOW + rows, HIGH)], h_send.at[1], h_recv.at[1], slab=prv)
-    up.start()
-    down.start()
-    send_levels_up = remote(lv_up, lv_up_in, h_send.at[2], h_recv.at[2], grid=up_z)
-    send_levels_down = remote(lv_down, lv_down_in, h_send.at[3], h_recv.at[3], grid=down_z)
-
-    @pl.when(z == 0)
+    inner_halo = remote(u_in.at[pl.ds(jnp.where(descending, rows - EDGE, 0), EDGE)],
+                        raw.at[pl.ds(jnp.where(descending, WIDE - EDGE, WIDE + rows), EDGE)],
+                        h_send.at[0], h_recv.at[0], slab=partner)
+    outer_halo = remote(u_in.at[pl.ds(jnp.where(descending, 0, rows - WIDE), WIDE)],
+                        raw.at[pl.ds(jnp.where(descending, WIDE + rows, 0), WIDE)],
+                        h_send.at[1], h_recv.at[1], slab=neighbour)
+    inner_halo.start()
+    outer_halo.start()
+    send_levels = remote(lv, lv_in, h_send.at[2], h_recv.at[2], grid=main_z)
+    share_levels = remote(lv, lv_in, h_send.at[3], h_recv.at[3], slab=partner)
+
+    @pl.when(hop == 0)
     def _():
-        send_levels_up.start()
-
-    @pl.when(z == Z - 1)
-    def _():
-        send_levels_down.start()
+        send_levels.start()
 
     loaded.wait()
 
-    @pl.when(descending)
-    def _():
-        down.wait_recv()
-
-    @pl.when(jnp.logical_not(descending))
-    def _():
-        up.wait_recv()
+    inner_halo.wait_recv()
 
     def raw_row(i):
-        r = LOW + row_of(descending, i)
+        r = WIDE + row_of(descending, i)
         return [raw[r, spot] for spot in spots()]
 
     warm_up(carry, [raw_row(i) for i in range(-STEPS, STEPS + 1)], coef)
 
     def first_cycle(j):
         m = march(carry, [raw_row(4 * j + 5 + i) for i in range(4)], coef)
-        r = 4 * group_of(descending, j)
-        coarse, one, two, three = surpluses(m, first_w, last_w, weight * keep_mid, weight * keep_fine)
-        put(terms, coarse, r)
-        put(terms, one, r + jnp.where(descending, 3, 1))
-        put(terms, two, r + 2)
-        put(terms, three, r + jnp.where(descending, 1, 3))
-
-    def chunk(i):
-        return pl.ds(4 * group_of(descending, i), 4)
-
-    def main_copy(i):
-        return remote(terms.at[chunk(i)], arrived.at[chunk(i)], ssem.at[i], rsem.at[i], grid=main_z)
-
-    halo_copy = remote(h_terms, h_arrived, h_send.at[4], h_recv.at[4], grid=halo_z)
+        four = surpluses(m, first_w, last_w, weight * keep_mid, weight * keep_fine)
+        order = [0, jnp.where(descending, 3, 1), 2, jnp.where(descending, 1, 3)]
+
+        @pl.when(j < groups)
+        def _():
+            for k, row in zip(order, four):
+                put(terms, row, 4 * group_of(descending, j) + k)
+
+        @pl.when(j == groups)
+        def _():
+            for k, row in zip(order, four):
+                put(o_terms, row, k + jnp.where(descending, 1, 0))
+            put(o_terms, [weight * x for x in m[4]], jnp.where(descending, 0, 4))
+
+    def piece(i, h):
+        return pl.ds(4 * group_of(descending, i) + PIECE * h, PIECE)
+
+    def main_copy(i, h):
+        return remote(terms.at[piece(i, h)], arrived.at[piece(i, h)], ssem.at[i, h], rsem.at[i, h], grid=main_z)
+
+    halo_copy = remote(h_terms, h_arrived, h_send.at[4], h_recv.at[4], grid=main_z)
+    halo_swap = remote(h_out, h_terms, h_send.at[8], h_recv.at[8], slab=partner)
+    outer_copy = remote(o_terms, o_arrived, h_send.at[6], h_recv.at[6], grid=main_z)
 
     def share_copy(i):
         where = pl.ds(OFF + 4 * group_of(region_desc, i), 4)
@@ -233,8 +240,6 @@
     inner = pl.ds(inner_at, EDGE)
     outer = pl.ds(outer_at, EDGE)
     share_inner = remote(sums.at[inner], sums.at[inner], h_send.at[5], h_recv.at[5], slab=partner)
-    swap_outer = remote(sums.at[pl.ds(OFF + jnp.where(region_desc, 0, rows - EDGE), EDGE)], sums.at[inner],
-                        h_send.at[6], h_recv.at[6], slab=neighbour)
     share_outer = remote(sums.at[outer], sums.at[outer], h_send.at[7], h_recv.at[7], slab=partner)
 
     def cell(q, keeps):
@@ -250,7 +255,7 @@
     def build_table():
         for n in range(local_grids):
             g = n + jnp.where(is_main, 0, local_grids)
-            both = jnp.where(z == 0, 1.0, 0.0) * lv_down[g] + jnp.where(z == 0, 0.0, 1.0) * lv_up[g]
+            both = jnp.where(is_main, 1.0, 0.0) * lv[g] + jnp.where(is_main, 0.0, 1.0) * lv_in[g]
             lines = [jnp.broadcast_to(both[d:d + 1], (8, lanes)) for d in range(6)]
             values = coefficients(lines[:5], region_desc)
             w = lines[5]
@@ -297,6 +302,12 @@
         return remote(fin.at[pl.ds(r, 4), x], whole.at[pl.ds(region * rows + r, 4)],
                       x_send.at[i, x], x_recv.at[i, chip], slab=2 * x + core)
 
+    def direct_copy(i, x, to, own, recv):
+        r = 4 * group_of(region_desc, i)
+        here = whole.at[pl.ds(region * rows + r, 4)]
+        return remote(here if own else fin.at[pl.ds(r, 4), x], here, all_send.at[i, x, to], recv.at[i, chip],
+                      grid=to, slab=2 * x + core)
+
     def slab_from(x, base):
         return 2 * x + (x % 2 if base == 0 else 1 - x % 2)
 
@@ -320,125 +331,125 @@
     start2 = reach + C2_LAG + 2
     swap_at = start2 + SWAP_LAG
     plane_at = swap_at + PLANE_LAG
-    last = plane_at + (Z - 1) * CHAIN_LAG + groups
+    last = max(swap_at + groups, plane_at + (Z - 2) * CHAIN_LAG + direct_from, plane_at + direct_from)
 
     @pl.loop(0, last)
     def _(j):
         @pl.when(j == groups - 2)
         def _():
-            @pl.when(descending)
-            def _():
-                up.wait_recv()
-
-            @pl.when(jnp.logical_not(descending))
-            def _():
-                down.wait_recv()
-
-        @pl.when(j < groups)
+            outer_halo.wait_recv()
+
+        @pl.when((hop == 0) & (j == 2))
+        def _():
+            halo_swap.wait_recv()
+            halo_copy.start()
+
+        @pl.when(j <= groups)
         def _():
             first_cycle(j)
 
-            @pl.when(hop == 0)
-            def _():
-                main_copy(j).start()
+            @pl.when((hop == 0) & (j < groups))
+            def _():
+                for h in range(4 // PIECE):
+                    main_copy(j, h).start()
+
+        @pl.when((hop == 0) & (j == groups))
+        def _():
+            outer_copy.start()
 
         @pl.when(j == 1)
         def _():
             e = jnp.where(descending, rows - EDGE, 0)
             for k in range(EDGE):
-                put(h_terms, get(terms, e + k), k)
-
-            @pl.when(h_hop == 0)
-            def _():
-                halo_copy.start()
-
-        @pl.when((z > 0) & (j == z * RS_LAG))
-        def _():
-            send_levels_up.wait_recv()
+                put(h_out, get(terms, e + k), k)
+            halo_swap.start()
+
+        @pl.when((hop > 0) & (j == hop * RS_LAG))
+        def _():
+            send_levels.wait_recv()
             for g in range(Z):
-                lv_up[g] = lv_up_in[g]
-            lv_up[z] = tile
-
-            @pl.when(z < Z - 1)
-            def _():
-                send_levels_up.start()
-
-        @pl.when((z < Z - 1) & (j == (Z - 1 - z) * RS_LAG))
-        def _():
-            send_levels_down.wait_recv()
-            for g in range(Z):
-                lv_down[g] = lv_down_in[g]
-            lv_down[z] = tile
-
-            @pl.when(z > 0)
-            def _():
-                send_levels_down.start()
-
-        @pl.when((h_hop > 0) & (j == 1 + h_hop * RS_LAG))
-        def _():
+                lv[g] = lv_in[g]
+            lv[z] = tile
+
+            @pl.when(hop < Z - 1)
+            def _():
+                send_levels.start()
+
+            @pl.when(hop == Z - 1)
+            def _():
+                share_levels.start()
+
+        b = j - hop * RS_LAG
+
+        @pl.when((hop > 0) & (b == 2))
+        def _():
+            halo_swap.wait_recv()
             halo_copy.wait_recv()
 
-            @pl.when(h_hop < Z - 1)
+            @pl.when(hop < Z - 1)
             def _():
                 for k in range(EDGE):
                     put(h_terms, [a + b for a, b in zip(get(h_terms, k), get(h_arrived, k))], k)
                 halo_copy.start()
 
-            @pl.when(h_hop == Z - 1)
+            @pl.when(hop == Z - 1)
             def _():
                 for k in range(EDGE):
                     put(sums, [a + b for a, b in zip(get(h_terms, k), get(h_arrived, k))], inner_at + k)
                 share_inner.start()
 
-        b = j - hop * RS_LAG
-
         @pl.when((hop > 0) & (b >= 0) & (b < groups))
         def _():
-            main_copy(b).wait_recv()
-            r = 4 * group_of(descending, b)
-
             @pl.when(hop < Z - 1)
             def _():
-                for k in range(4):
-                    put(terms, [a + c for a, c in zip(get(terms, r + k), get(arrived, r + k))], r + k)
-                main_copy(b).start()
+                for h in range(4 // PIECE):
+                    r = 4 * group_of(descending, b) + h * PIECE
+                    main_copy(b, h).wait_recv()
+                    for k in range(PIECE):
+                        put(terms, [a + c for a, c in zip(get(terms, r + k), get(arrived, r + k))], r + k)
+                    main_copy(b, h).start()
 
             @pl.when(hop == Z - 1)
             def _():
-                for k in range(4):
-                    put(sums, [a + c for a, c in zip(get(terms, r + k), get(arrived, r + k))], OFF + r + k)
+                for h in range(4 // PIECE):
+                    r = 4 * group_of(descending, b) + h * PIECE
+                    main_copy(b, h).wait_recv()
+                    for k in range(PIECE):
+                        put(sums, [a + c for a, c in zip(get(terms, r + k), get(arrived, r + k))], OFF + r + k)
                 share_copy(b).start()
 
-                @pl.when(b == groups - 1)
-                def _():
-                    swap_outer.start()
+        @pl.when((hop > 0) & (b == groups))
+        def _():
+            outer_copy.wait_recv()
+
+            @pl.when(hop < Z - 1)
+            def _():
+                for k in range(EDGE):
+                    put(o_terms, [a + c for a, c in zip(get(o_terms, k), get(o_arrived, k))], k)
+                outer_copy.start()
+
+            @pl.when(hop == Z - 1)
+            def _():
+                for k in range(EDGE):
+                    put(sums, [a + c for a, c in zip(get(o_terms, k), get(o_arrived, k))], outer_at + k)
+                share_outer.start()
 
         i = j - start2
 
         @pl.when(at_end & (i == 0))
         def _():
-            build_table()
-
-            @pl.when(is_main)
-            def _():
+            @pl.when(jnp.logical_not(is_main))
+            def _():
+                share_levels.wait_recv()
                 share_inner.wait_recv()
-
-            @pl.when(jnp.logical_not(is_main))
-            def _():
                 for k in range(min(2, groups)):
                     share_copy(k).wait_recv()
+            build_table()
             second_warm()
 
-        @pl.when(at_end & (i == groups - 2))
-        def _():
-            @pl.when(is_main)
-            def _():
-                swap_outer.wait_recv()
-                share_outer.start()
-
-            @pl.when(jnp.logical_not(is_main))
-            def _():
-                share_outer.wait_recv()
+        @pl.when(at_end & jnp.logical_not(is_main) & (i == groups - 2))
+        def _():
+            share_outer.wait_recv()
 
         @pl.when(at_end & (i >= 0) & (i < groups))
         def _():
@@ -468,9 +479,32 @@
                         fin[r + n, x] = part[r + n, quarter(x, core)] + swapped[r + n, x]
                     plane_copy(k, x).start()
 
+            @pl.when(k >= direct_from)
+            def _():
+                @pl.loop(1, Z)
+                def _(away):
+                    for x in range(chips):
+                        to = jnp.where(z == 0, Z - away, away - 1)
+
+                        @pl.when((z == 0) & (chip == x))
+                        def _():
+                            direct_copy(k, x, to, True, up_recv).start()
+
+                        @pl.when((z == 0) & (chip != x))
+                        def _():
+                            direct_copy(k, x, to, False, up_recv).start()
+
+                        @pl.when((z > 0) & (chip == x))
+                        def _():
+                            direct_copy(k, x, to, True, dn_recv).start()
+
+                        @pl.when((z > 0) & (chip != x))
+                        def _():
+                            direct_copy(k, x, to, False, dn_recv).start()
+
         k2 = j - plane_at
 
-        @pl.when((z == 0) & (k2 >= 0) & (k2 < groups))
+        @pl.when((z == 0) & (k2 >= 0) & (k2 < direct_from))
         def _():
             for x in range(chips):
                 @pl.when(chip != x)
@@ -478,7 +512,7 @@
                     plane_arrival(k2, x, 0).wait_recv()
                 up_copy(k2, x).start()
 
-        @pl.when((z == Z - 1) & (k2 >= 0) & (k2 < groups))
+        @pl.when((z == Z - 1) & (k2 >= 0) & (k2 < direct_from))
         def _():
             for x in range(chips):
                 @pl.when(chip != x)
@@ -488,31 +522,61 @@
 
         f = k2 - z * CHAIN_LAG
 
-        @pl.when((z > 0) & (f >= 0) & (f < groups))
+        @pl.when((z > 0) & (z < Z - 1) & (f >= 0) & (f < direct_from))
         def _():
             for x in range(chips):
                 up_copy(f, x).wait_recv()
-
-                @pl.when(z < Z - 1)
-                def _():
-                    up_copy(f, x).start()
+                up_copy(f, x).start()
 
         d = k2 - (Z - 1 - z) * CHAIN_LAG
 
-        @pl.when((z < Z - 1) & (d >= 0) & (d < groups))
+        @pl.when((z < Z - 1) & (z > 0) & (d >= 0) & (d < direct_from))
         def _():
             for x in range(chips):
                 down_copy(d, x).wait_recv()
-
-                @pl.when(z > 0)
-                def _():
-                    down_copy(d, x).start()
+                down_copy(d, x).start()
+
+    @pl.loop(0, groups)
+    def _(i):
+        for x in range(chips):
+            @pl.when((z == Z - 1) | ((z > 0) & (i >= direct_from)))
+            def _():
+                up_copy(i, x).wait_recv()
+
+            @pl.when((z == 0) | ((z < Z - 1) & (i >= direct_from)))
+            def _():
+                down_copy(i, x).wait_recv()
+
+            @pl.when((z == 0) & (chip != x) & (i >= direct_from))
+            def _():
+                plane_arrival(i, x, 0).wait_recv()
+
+            @pl.when((z == Z - 1) & (chip != x) & (i >= direct_from))
+            def _():
+                plane_arrival(i, x, 1).wait_recv()
+
+    owners.wait()
+
+    def nodal(i):
+        return coarse[i // 4]
+
+    for i in range(0, count, 4):
+        coarse[i // 4] = whole[i]
+    for spacing in [1 << t for t in range(2, count.bit_length() - 1)]:
+        for i in range(spacing, count, 2 * spacing):
+            coarse[i // 4] = nodal(i) - 0.5 * (nodal(i - spacing) + nodal((i + spacing) % count))
+
+    for r in range(owned):
+        position = owner[z * owned + r]
+        top = jnp.where(position % 4 == 0, jnp.float32(1.0), jnp.float32(0.0))
+        out[r] = top * coarse[position // 4] + (1.0 - top) * whole[position]
 
     @pl.loop(0, groups)
     def _(i):
         @pl.when(hop < Z - 1)
         def _():
-            main_copy(i).wait_send()
+            for h in range(4 // PIECE):
+                main_copy(i, h).wait_send()
 
         @pl.when(at_end & is_main)
         def _():
@@ -527,45 +591,36 @@
             def _():
                 plane_copy(i, x).wait_send()
 
-            @pl.when(z < Z - 1)
+            @pl.when((z < Z - 1) & (i < direct_from))
             def _():
                 up_copy(i, x).wait_send()
 
-            @pl.when(z > 0)
+            @pl.when((z > 0) & (i < direct_from))
             def _():
                 down_copy(i, x).wait_send()
 
-    up.wait_send()
-    down.wait_send()
-
-    @pl.when(h_hop < Z - 1)
+            @pl.when(at_end & (i >= direct_from))
+            def _():
+                @pl.loop(1, Z)
+                def _(away):
+                    to = jnp.where(z == 0, Z - away, away - 1)
+                    direct_copy(i, x, to, False, up_recv).wait_send()
+
+    inner_halo.wait_send()
+    outer_halo.wait_send()
+    halo_swap.wait_send()
+
+    @pl.when(hop < Z - 1)
     def _():
         halo_copy.wait_send()
-
-    @pl.when(z < Z - 1)
-    def _():
-        send_levels_up.wait_send()
-
-    @pl.when(z > 0)
-    def _():
-        send_levels_down.wait_send()
+        outer_copy.wait_send()
+        send_levels.wait_send()
 
     @pl.when(at_end & is_main)
     def _():
-        swap_outer.wait_send()
+        share_levels.wait_send()
+        share_inner.wait_send()
         share_outer.wait_send()
-
-    @pl.when(at_end & jnp.logical_not(is_main))
-    def _():
-        share_inner.wait_send()
-
-    for spacing in [1 << t for t in range(2, count.bit_length() - 1)]:
-        for i in range(spacing, count, 2 * spacing):
-            whole[i] = whole[i] - 0.5 * (whole[i - spacing] + whole[(i + spacing) % count])
-
-    @pl.loop(0, owned)
-    def _(r):
-        out[r] = whole[owner[z * owned + r]]
 
 
 def local(field, levels, owner):
@@ -581,21 +636,24 @@
     vmem = lambda *shape: pltpu.VMEM(shape, jnp.float32)
     sems = lambda *shape: pltpu.SemaphoreType.DMA(shape)
     level_tiles = vmem(Z, 8, lanes)
+    hbm = pl.BlockSpec(memory_space=pltpu.HBM)
     return pl.pallas_call(
         functools.partial(kernel, (Z, S, rows, count, lanes)),
         out_shape=jax.ShapeDtypeStruct((owned, width, lanes), jnp.float32),
-        in_specs=[pl.BlockSpec(memory_space=pltpu.SMEM), pl.BlockSpec(memory_space=pltpu.SMEM),
-                  pl.BlockSpec(memory_space=pl.ANY)],
+        in_specs=[hbm, hbm, hbm],
         out_specs=pl.BlockSpec(memory_space=pltpu.VMEM),
         scratch_shapes=[
-            vmem(rows + LOW + HIGH, flat, lanes), vmem(STEPS + 1, 2, *tail), vmem(rows, *tail), vmem(rows, *tail),
+            pltpu.SMEM(levels.shape, jnp.int32), pltpu.SMEM(owner.shape, jnp.int32),
+            vmem(rows + 2 * WIDE, flat, lanes), vmem(STEPS + 1, 2, *tail), vmem(rows, *tail), vmem(rows, *tail),
+            vmem(EDGE, *tail), vmem(EDGE, *tail), vmem(EDGE, *tail),
             vmem(EDGE, *tail), vmem(EDGE, *tail), vmem(OFF + rows + EDGE, *tail),
             vmem(grids, STEPS + 1, 2, *tail), vmem(rows, flat, lanes), vmem(rows, chips, width, lanes),
-            vmem(rows, chips, width, lanes), vmem(count, width, lanes), vmem(grids, 19, 8, lanes),
-            level_tiles, level_tiles, level_tiles, level_tiles,
-            sems(groups), sems(groups), sems(groups), sems(groups), sems(groups, chips), sems(groups, chips),
+            vmem(rows, chips, width, lanes), vmem(count, width, lanes), vmem(count // 4, width, lanes),
+            vmem(grids, 19, 8, lanes), level_tiles, level_tiles,
+            sems(groups, 4 // PIECE), sems(groups, 4 // PIECE), sems(groups), sems(groups),
             sems(groups, chips), sems(groups, chips), sems(groups, chips), sems(groups, chips),
-            sems(groups, chips), sems(groups, chips), sems(8), sems(8), pltpu.SemaphoreType.DMA,
+            sems(groups, chips), sems(groups, chips), sems(groups, chips), sems(groups, chips),
+            sems(groups, chips, Z), sems(10), sems(10), sems(3),
         ],
         compiler_params=pltpu.CompilerParams(collective_id=0, has_side_effects=True,
                                              vmem_limit_bytes=40 * 1024 * 1024),

time: 72.6 us -> 59.6 us (0.82)
  Pallas kernels: 69.8 us -> 56.8 us
    pallas_call x1, Pallas kernels: 69.8 us -> 56.8 us  [local(): pl.pallas_call(functools.partial(kernel, (Z, S, rows, count, lanes)), out...]
where the time goes in v2:
time: 59.6 us; the launch traced here: 59.4 us
  Pallas kernels  56.8 us (95%)
  local copies, waits for them, and re-layouts  2.6 us (4%)
    pallas_call x1, Pallas kernels, local(): pl.pallas_call(functools.partial(kernel, (Z, S, rows, count, lanes)), out...  56.8 us
    unnamed x7, local copies, waits for them, and re-layouts  2.6 us

profile of v2, /device:TPU:0, one launch (start us, length us, event | category | flops | bytes accessed | tf_op | source)
XLA Modules:
  0.0 59.4 jit_solution(6700026478236360249)
XLA Ops:
  0.0 0.0 copy-start.2
  0.0 0.0 copy-start.1
  0.0 0.7 %copy-done.2 = s32[128]{0:T(128)S(1)} copy-done((s32[128]{0:T(128)S(1)}, s32[128]{0:T(128)}, u32[]{:S(2)}) %copy-start.2) | copy-done | bytes 536
  0.7 0.0 copy-done.1
  0.7 0.0 copy-start
  0.7 1.2 %copy-done = f32[1,32,64,128]{3,2,1,0:T(8,128)S(1)} copy-done((f32[1,32,64,128]{3,2,1,0:T(8,128)S(1)}, f32[1,32,64,128]{3,2,1,0:T(8,128)}, u32[]{:S(2)}) %copy-start) | copy-done | bytes 1048600
  1.9 56.8 %shard_map.37 = f32[32,16,128]{2,1,0:T(8,128)S(1)} custom-call(s32[1,5]{1,0:T(1,128)S(1)} %copy-done.1, s32[128]{0:T(128)S(1)} %copy-done.2, f32[32,64,128]{2,1,0:T(8,128)S(1)} %bitcast.1), custom_call_target="tpu_custom_call" | custom-call | tf_op jit(solution)/shard_map/pallas_call | solution.py:640
  58.7 0.7 %copy.5 = f32[32,16,128]{2,1,0:T(8,128)} copy(f32[32,16,128]{2,1,0:T(8,128)S(1)} %shard_map.37) | data formatting | bytes 524288
Async XLA Ops:
  0.0 0.7 %copy-start.2 = (s32[128]{0:T(128)S(1)}, s32[128]{0:T(128)}, u32[]{:S(2)}) copy-start(s32[128]{0:T(128)} %owner_in.1) | copy-start | bytes 1540
  0.0 0.7 %copy-start.1 = (s32[1,5]{1,0:T(1,128)S(1)}, s32[1,5]{1,0:T(1,128)}, u32[]{:S(2)}) copy-start(s32[1,5]{1,0:T(1,128)} %levels_in.1) | copy-start | bytes 64
  0.7 1.2 %copy-start = (f32[1,32,64,128]{3,2,1,0:T(8,128)S(1)}, f32[1,32,64,128]{3,2,1,0:T(8,128)}, u32[]{:S(2)}) copy-start(f32[1,32,64,128]{3,2,1,0:T(8,128)} %param.3) | copy-start | bytes 3145732

commit v3 on v2

--- a/solution.py
+++ b/solution.py
@@ -106,7 +106,7 @@
 
 def kernel(sizes, levels_in, owner_in, u_in, out, levels, owner, raw, carry, terms, arrived, h_out, h_terms, h_arrived, o_terms, o_arrived,
            sums, carry2, part, swapped, fin, whole, coarse, table, lv, lv_in,
-           ssem, rsem, c_send, c_recv, p_send, p_recv, x_send, x_recv, up_send, up_recv, dn_send, dn_recv, all_send,
+           ssem, rsem, c_send, c_recv, p_send, p_recv, x_send, x_recv, up_send, up_recv, dn_send, dn_recv, all_send, e_send, e_recv,
            h_send, h_recv, in_sem):
     Z, S, rows, count, lanes = sizes
     flat = N1 * N2 * N3
@@ -161,6 +161,16 @@
     def _():
         pl.semaphore_signal(barrier, inc=1, device_id={"grid": up_z}, device_id_type=MESH)
 
+    pl.semaphore_wait(barrier, S - 1 + jnp.where(z > 0, 1, 0) + jnp.where(z < Z - 1, 1, 0))
+
+    inner_halo = remote(u_in.at[pl.ds(jnp.where(descending, rows - EDGE, 0), EDGE)],
+                        raw.at[pl.ds(jnp.where(descending, WIDE - EDGE, WIDE + rows), EDGE)],
+                        h_send.at[0], h_recv.at[0], slab=partner)
+    outer_halo = remote(u_in.at[pl.ds(jnp.where(descending, 0, rows - WIDE), WIDE)],
+                        raw.at[pl.ds(jnp.where(descending, WIDE + rows, 0), WIDE)],
+                        h_send.at[1], h_recv.at[1], slab=neighbour)
+    inner_halo.start()
+    outer_halo.start()
     small.wait()
     vec = [levels[0, d] for d in range(5)]
     scales = [lax.shift_left(jnp.int32(1), v).astype(jnp.float32) * 0.125 for v in vec]
@@ -178,16 +188,6 @@
     first_w = jnp.where(descending, 0.0 * weight, weight)
     last_w = jnp.where(descending, weight, 0.0 * weight)
 
-    pl.semaphore_wait(barrier, S - 1 + jnp.where(z > 0, 1, 0) + jnp.where(z < Z - 1, 1, 0))
-
-    inner_halo = remote(u_in.at[pl.ds(jnp.where(descending, rows - EDGE, 0), EDGE)],
-                        raw.at[pl.ds(jnp.where(descending, WIDE - EDGE, WIDE + rows), EDGE)],
-                        h_send.at[0], h_recv.at[0], slab=partner)
-    outer_halo = remote(u_in.at[pl.ds(jnp.where(descending, 0, rows - WIDE), WIDE)],
-                        raw.at[pl.ds(jnp.where(descending, WIDE + rows, 0), WIDE)],
-                        h_send.at[1], h_recv.at[1], slab=neighbour)
-    inner_halo.start()
-    outer_halo.start()
     send_levels = remote(lv, lv_in, h_send.at[2], h_recv.at[2], grid=main_z)
     share_levels = remote(lv, lv_in, h_send.at[3], h_recv.at[3], slab=partner)
 
@@ -227,9 +227,13 @@
     def main_copy(i, h):
         return remote(terms.at[piece(i, h)], arrived.at[piece(i, h)], ssem.at[i, h], rsem.at[i, h], grid=main_z)
 
-    halo_copy = remote(h_terms, h_arrived, h_send.at[4], h_recv.at[4], grid=main_z)
+    def halo_copy(k):
+        return remote(h_terms.at[k], h_arrived.at[k], e_send.at[0, k], e_recv.at[0, k], grid=main_z)
+
+    def outer_copy(k):
+        return remote(o_terms.at[k], o_arrived.at[k], e_send.at[1, k], e_recv.at[1, k], grid=main_z)
+
     halo_swap = remote(h_out, h_terms, h_send.at[8], h_recv.at[8], slab=partner)
-    outer_copy = remote(o_terms, o_arrived, h_send.at[6], h_recv.at[6], grid=main_z)
 
     def share_copy(i):
         where = pl.ds(OFF + 4 * group_of(region_desc, i), 4)
@@ -331,7 +335,7 @@
     start2 = reach + C2_LAG + 2
     swap_at = start2 + SWAP_LAG
     plane_at = swap_at + PLANE_LAG
-    last = max(swap_at + groups, plane_at + (Z - 2) * CHAIN_LAG + direct_from, plane_at + direct_from)
+    last = max(plane_at + groups, plane_at + (Z - 2) * CHAIN_LAG + direct_from)
 
     @pl.loop(0, last)
     def _(j):
@@ -342,7 +346,8 @@
         @pl.when((hop == 0) & (j == 2))
         def _():
             halo_swap.wait_recv()
-            halo_copy.start()
+            for k in range(EDGE):
+                halo_copy(k).start()
 
         @pl.when(j <= groups)
         def _():
@@ -355,7 +360,8 @@
 
         @pl.when((hop == 0) & (j == groups))
         def _():
-            outer_copy.start()
+            for k in range(EDGE):
+                outer_copy(k).start()
 
         @pl.when(j == 1)
         def _():
@@ -384,17 +390,17 @@
         @pl.when((hop > 0) & (b == 2))
         def _():
             halo_swap.wait_recv()
-            halo_copy.wait_recv()
-
             @pl.when(hop < Z - 1)
             def _():
                 for k in range(EDGE):
+                    halo_copy(k).wait_recv()
                     put(h_terms, [a + b for a, b in zip(get(h_terms, k), get(h_arrived, k))], k)
-                halo_copy.start()
+                    halo_copy(k).start()
 
             @pl.when(hop == Z - 1)
             def _():
                 for k in range(EDGE):
+                    halo_copy(k).wait_recv()
                     put(sums, [a + b for a, b in zip(get(h_terms, k), get(h_arrived, k))], inner_at + k)
                 share_inner.start()
 
@@ -420,17 +426,17 @@
 
         @pl.when((hop > 0) & (b == groups))
         def _():
-            outer_copy.wait_recv()
-
             @pl.when(hop < Z - 1)
             def _():
                 for k in range(EDGE):
+                    outer_copy(k).wait_recv()
                     put(o_terms, [a + c for a, c in zip(get(o_terms, k), get(o_arrived, k))], k)
-                outer_copy.start()
+                    outer_copy(k).start()
 
             @pl.when(hop == Z - 1)
             def _():
                 for k in range(EDGE):
+                    outer_copy(k).wait_recv()
                     put(sums, [a + c for a, c in zip(get(o_terms, k), get(o_arrived, k))], outer_at + k)
                 share_outer.start()
 
@@ -479,29 +485,6 @@
                         fin[r + n, x] = part[r + n, quarter(x, core)] + swapped[r + n, x]
                     plane_copy(k, x).start()
 
-            @pl.when(k >= direct_from)
-            def _():
-                @pl.loop(1, Z)
-                def _(away):
-                    for x in range(chips):
-                        to = jnp.where(z == 0, Z - away, away - 1)
-
-                        @pl.when((z == 0) & (chip == x))
-                        def _():
-                            direct_copy(k, x, to, True, up_recv).start()
-
-                        @pl.when((z == 0) & (chip != x))
-                        def _():
-                            direct_copy(k, x, to, False, up_recv).start()
-
-                        @pl.when((z > 0) & (chip == x))
-                        def _():
-                            direct_copy(k, x, to, True, dn_recv).start()
-
-                        @pl.when((z > 0) & (chip != x))
-                        def _():
-                            direct_copy(k, x, to, False, dn_recv).start()
-
         k2 = j - plane_at
 
         @pl.when((z == 0) & (k2 >= 0) & (k2 < direct_from))
@@ -520,6 +503,29 @@
                     plane_arrival(k2, x, 1).wait_recv()
                 down_copy(k2, x).start()
 
+        @pl.when(at_end & (k2 >= direct_from) & (k2 < groups))
+        def _():
+            @pl.loop(1, Z)
+            def _(away):
+                for x in range(chips):
+                    to = jnp.where(z == 0, Z - away, away - 1)
+
+                    @pl.when((z == 0) & (chip == x))
+                    def _():
+                        direct_copy(k2, x, to, True, up_recv).start()
+
+                    @pl.when((z == 0) & (chip != x))
+                    def _():
+                        direct_copy(k2, x, to, False, up_recv).start()
+
+                    @pl.when((z > 0) & (chip == x))
+                    def _():
+                        direct_copy(k2, x, to, True, dn_recv).start()
+
+                    @pl.when((z > 0) & (chip != x))
+                    def _():
+                        direct_copy(k2, x, to, False, dn_recv).start()
+
         f = k2 - z * CHAIN_LAG
 
         @pl.when((z > 0) & (z < Z - 1) & (f >= 0) & (f < direct_from))
@@ -535,6 +541,60 @@
             for x in range(chips):
                 down_copy(d, x).wait_recv()
                 down_copy(d, x).start()
+
+    @pl.loop(0, groups)
+    def _(i):
+        @pl.when(hop < Z - 1)
+        def _():
+            for h in range(4 // PIECE):
+                main_copy(i, h).wait_send()
+
+        @pl.when(at_end & is_main)
+        def _():
+            share_copy(i).wait_send()
+
+        for x in range(chips):
+            @pl.when(at_end)
+            def _():
+                swap_copy(i, x).wait_send()
+
+            @pl.when(at_end & (chip != x))
+            def _():
+                plane_copy(i, x).wait_send()
+
+            @pl.when((z < Z - 1) & (i < direct_from))
+            def _():
+                up_copy(i, x).wait_send()
+
+            @pl.when((z > 0) & (i < direct_from))
+            def _():
+                down_copy(i, x).wait_send()
+
+            @pl.when(at_end & (i >= direct_from))
+            def _():
+                @pl.loop(1, Z)
+                def _(away):
+                    to = jnp.where(z == 0, Z - away, away - 1)
+                    direct_copy(i, x, to, False, up_recv).wait_send()
+
+    inner_halo.wait_send()
+    outer_halo.wait_send()
+    halo_swap.wait_send()
+
+    @pl.when(hop < Z - 1)
+    def _():
+        for k in range(EDGE):
+            halo_copy(k).wait_send()
+            outer_copy(k).wait_send()
+        send_levels.wait_send()
+
+    @pl.when(at_end & is_main)
+    def _():
+        share_levels.wait_send()
+        share_inner.wait_send()
+        share_outer.wait_send()
+
+    owners.wait()
 
     @pl.loop(0, groups)
     def _(i):
@@ -554,8 +614,6 @@
             @pl.when((z == Z - 1) & (chip != x) & (i >= direct_from))
             def _():
                 plane_arrival(i, x, 1).wait_recv()
-
-    owners.wait()
 
     def nodal(i):
         return coarse[i // 4]
@@ -570,57 +628,6 @@
         position = owner[z * owned + r]
         top = jnp.where(position % 4 == 0, jnp.float32(1.0), jnp.float32(0.0))
         out[r] = top * coarse[position // 4] + (1.0 - top) * whole[position]
-
-    @pl.loop(0, groups)
-    def _(i):
-        @pl.when(hop < Z - 1)
-        def _():
-            for h in range(4 // PIECE):
-                main_copy(i, h).wait_send()
-
-        @pl.when(at_end & is_main)
-        def _():
-            share_copy(i).wait_send()
-
-        for x in range(chips):
-            @pl.when(at_end)
-            def _():
-                swap_copy(i, x).wait_send()
-
-            @pl.when(at_end & (chip != x))
-            def _():
-                plane_copy(i, x).wait_send()
-
-            @pl.when((z < Z - 1) & (i < direct_from))
-            def _():
-                up_copy(i, x).wait_send()
-
-            @pl.when((z > 0) & (i < direct_from))
-            def _():
-                down_copy(i, x).wait_send()
-
-            @pl.when(at_end & (i >= direct_from))
-            def _():
-                @pl.loop(1, Z)
-                def _(away):
-                    to = jnp.where(z == 0, Z - away, away - 1)
-                    direct_copy(i, x, to, False, up_recv).wait_send()
-
-    inner_halo.wait_send()
-    outer_halo.wait_send()
-    halo_swap.wait_send()
-
-    @pl.when(hop < Z - 1)
-    def _():
-        halo_copy.wait_send()
-        outer_copy.wait_send()
-        send_levels.wait_send()
-
-    @pl.when(at_end & is_main)
-    def _():
-        share_levels.wait_send()
-        share_inner.wait_send()
-        share_outer.wait_send()
 
 
 def local(field, levels, owner):
@@ -653,7 +660,7 @@
             sems(groups, 4 // PIECE), sems(groups, 4 // PIECE), sems(groups), sems(groups),
             sems(groups, chips), sems(groups, chips), sems(groups, chips), sems(groups, chips),
             sems(groups, chips), sems(groups, chips), sems(groups, chips), sems(groups, chips),
-            sems(groups, chips, Z), sems(10), sems(10), sems(3),
+            sems(groups, chips, Z), sems(2, EDGE), sems(2, EDGE), sems(10), sems(10), sems(3),
         ],
         compiler_params=pltpu.CompilerParams(collective_id=0, has_side_effects=True,
                                              vmem_limit_bytes=40 * 1024 * 1024),

time: 59.6 us -> 57.8 us (0.970)
  Pallas kernels: 56.8 us -> 55 us
    pallas_call x1, Pallas kernels: 56.8 us -> 55 us  [local(): pl.pallas_call(functools.partial(kernel, (Z, S, rows, count, lanes)), out...]
where the time goes in v3:
time: 57.8 us; the launch traced here: 57.7 us
  Pallas kernels  55 us (95%)
  local copies, waits for them, and re-layouts  2.6 us (4%)
    pallas_call x1, Pallas kernels, local(): pl.pallas_call(functools.partial(kernel, (Z, S, rows, count, lanes)), out...  55 us
    unnamed x7, local copies, waits for them, and re-layouts  2.6 us

profile of v3, /device:TPU:0, one launch (start us, length us, event | category | flops | bytes accessed | tf_op | source)
XLA Modules:
  0.0 57.7 jit_solution(9458950403912533654)
XLA Ops:
  0.0 0.0 copy-start.2
  0.0 0.0 copy-start.1
  0.0 0.7 %copy-done.2 = s32[128]{0:T(128)S(1)} copy-done((s32[128]{0:T(128)S(1)}, s32[128]{0:T(128)}, u32[]{:S(2)}) %copy-start.2) | copy-done | bytes 536
  0.7 0.0 copy-done.1
  0.7 0.0 copy-start
  0.7 1.2 %copy-done = f32[1,32,64,128]{3,2,1,0:T(8,128)S(1)} copy-done((f32[1,32,64,128]{3,2,1,0:T(8,128)S(1)}, f32[1,32,64,128]{3,2,1,0:T(8,128)}, u32[]{:S(2)}) %copy-start) | copy-done | bytes 1048600
  1.9 55.0 %shard_map.37 = f32[32,16,128]{2,1,0:T(8,128)S(1)} custom-call(s32[1,5]{1,0:T(1,128)S(1)} %copy-done.1, s32[128]{0:T(128)S(1)} %copy-done.2, f32[32,64,128]{2,1,0:T(8,128)S(1)} %bitcast.1), custom_call_target="tpu_custom_call" | custom-call | tf_op jit(solution)/shard_map/pallas_call | solution.py:647
  56.9 0.7 %copy.5 = f32[32,16,128]{2,1,0:T(8,128)} copy(f32[32,16,128]{2,1,0:T(8,128)S(1)} %shard_map.37) | data formatting | bytes 524288
Async XLA Ops:
  0.0 0.7 %copy-start.2 = (s32[128]{0:T(128)S(1)}, s32[128]{0:T(128)}, u32[]{:S(2)}) copy-start(s32[128]{0:T(128)} %owner_in.1) | copy-start | bytes 1540
  0.0 0.7 %copy-start.1 = (s32[1,5]{1,0:T(1,128)S(1)}, s32[1,5]{1,0:T(1,128)}, u32[]{:S(2)}) copy-start(s32[1,5]{1,0:T(1,128)} %levels_in.1) | copy-start | bytes 64
  0.7 1.2 %copy-start = (f32[1,32,64,128]{3,2,1,0:T(8,128)S(1)}, f32[1,32,64,128]{3,2,1,0:T(8,128)}, u32[]{:S(2)}) copy-start(f32[1,32,64,128]{3,2,1,0:T(8,128)} %param.3) | copy-start | bytes 3145732
